TPU v7x, 256 devices: a whole 4x4x8 slice. The times are simulated.
256 devices in a mesh: row: 16 (over z, core), col: 16 (over y, x).
Axes of the slice: x: 4, y: 4, z: 8, core: 2. Of those that a mesh axis runs over, the one named last changes fastest.
Arguments:
- act_codes: int32 [2048, 7168], P('col', 'row'), may hold values from -127 to 127
- act_scales: float32 [2048, 112], P('col', 'row'), may hold values from 0.005 to 0.03
- gate_weight: bfloat16 [7168, 18432], P('row', 'col'), may hold values from -0.0625 to 0.0625
- up_weight: bfloat16 [7168, 18432], P('row', 'col'), may hold values from -0.0625 to 0.0625
- down_weight: bfloat16 [18432, 7168], P('col', 'row'), may hold values from -0.046875 to 0.046875
Outputs:
- mixed: bfloat16 [2048, 7168], P('col', 'row')
All inputs are finite; a program needn't handle non-finite values.
Results may differ from a plain program's by a relative error of at most 0.03.
Values may be sent and summed in bfloat16 or wider, within the bound.
A program may use at most 128 MiB of HBM per device.

v0:
```python
import jax
import jax.numpy as jnp
from jax import lax
from jax.sharding import Mesh
from jax.sharding import PartitionSpec as P

ROW = ("row_0", "row_1")


def in_order(tiles, dim):
    tiles = jnp.moveaxis(tiles, 0, dim)
    lengths = tiles.shape
    return tiles.reshape(*lengths[:dim], lengths[dim] * lengths[dim + 1], *lengths[dim + 2 :])


def sent_to_all(array, axis):
    copies = jnp.broadcast_to(array, (lax.axis_size(axis), *array.shape))
    return lax.all_to_all(copies, axis, split_axis=0, concat_axis=0, tiled=True)


def gather_directly(array, axis, dim):
    return in_order(sent_to_all(array, axis), dim)


def own_block(tiles, axes, order):
    lengths = [lax.axis_size(a) for a in axes]
    tiles = tiles.reshape(*lengths, *tiles.shape[1:])
    tiles = tiles.transpose(*order, *range(len(axes), tiles.ndim))
    tiles = tiles.reshape(-1, *tiles.shape[len(axes) :])
    for k in order:
        tiles = lax.psum_scatter(tiles, axes[k], scatter_dimension=0, tiled=True)
    return tiles[0]


def cut_along(array, dim, length):
    before, after = (array.shape[:dim], array.shape[dim + 1 :])
    return jnp.moveaxis(array.reshape(*before, length, -1, *after), dim, 0)


def scatter_axes(array, axes, order, dim):
    length = lax.axis_size(axes)
    return own_block(cut_along(array, dim, length), axes, order)


def sent_and_summed(array, axis, dim):
    length = lax.axis_size(axis)
    tiles = lax.all_to_all(cut_along(array, dim, length), axis, 0, 0, tiled=True)
    return jnp.sum(tiles.astype(jnp.float32), axis=0)


def on_device(act_codes, act_scales, gate_weight, up_weight, down_weight):
    local_rows = act_codes.shape[0]
    width = act_codes.shape[1]
    nblocks = act_scales.shape[1]
    blocked = act_codes.astype(jnp.float32).reshape(local_rows, nblocks, width // nblocks)
    acts = (blocked * act_scales[:, :, None]).reshape(local_rows, width).astype(jnp.bfloat16)
    every = gather_directly(acts, "col", 0)
    hidden_width = gate_weight.shape[1]
    gate_part = jnp.dot(every, gate_weight, preferred_element_type=jnp.float32)
    up_part = jnp.dot(every, up_weight, preferred_element_type=jnp.float32)
    summed = scatter_axes(
        jnp.concatenate([gate_part, up_part], axis=1).astype(jnp.bfloat16), ROW, (1, 0), 0
    ).astype(jnp.float32)
    hidden = (jax.nn.silu(summed[:, :hidden_width]) * summed[:, hidden_width:]).astype(jnp.bfloat16)
    partial_value = jnp.dot(
        lax.all_gather(hidden, ROW, axis=0, tiled=True),
        down_weight,
        preferred_element_type=jnp.float32,
    )
    mixed = sent_and_summed(partial_value.astype(jnp.bfloat16), "col", 0)
    return mixed.astype(jnp.bfloat16)


def solution(mesh):
    torus = Mesh(mesh.devices.reshape(8, 2, mesh.shape["col"]), ("row_0", "row_1", "col"))
    in_specs = (P("col", ROW), P("col", ROW), P(ROW, "col"), P(ROW, "col"), P("col", ROW))
    out_specs = P("col", ROW)
    return jax.shard_map(
        on_device, mesh=torus, in_specs=in_specs, out_specs=out_specs, check_vma=False
    )
```

profile of v0, /device:TPU:1, one launch (start us, length us, event | category | flops | bytes accessed | tf_op | source)
XLA Modules:
  0.0 233.5 jit_solution(17031267609659101783)
XLA Ops:
  6.5 0.0 copy-start
  6.5 0.0 reduce-scatter.3.cloned.1.call-start
  6.5 1.1 fusion.4
  7.6 0.3 broadcast_in_dim.4
  8.0 32.1 %all_to_all.10 = bf16[16,128,448]{1,2,0:T(8,128)(2,1)S(1)} all-to-all(bf16[16,128,448]{1,2,0:T(8,128)(2,1)S(1)} %broadcast_in_dim.4), channel_id=1, replica_groups=mesh['row_0'=8,'row_1'=2,'col'=16] {'col'}, dimensions={0} | all-to-all | bytes 3670016 | tf_op jit(solution)/shard_map/all_to_all | solution.py:18
  40.1 0.0 copy-start.1
  40.1 0.0 copy-done
  40.1 3.2 %convolution_convert_fusion = bf16[8,2,128,1152]{3,2,1,0:T(8,128)(2,1)S(1)} fusion(bf16[8,2,128,448]{2,3,1,0:T(8,128)(2,1)S(1)} %bitcast.32, bf16[448,1152]{1,0:T(8,128)(2,1)S(1)} %copy-done), kind=kOutput, calls=%fused_computation.1 | convolution fusion | flops 2116288512 | bytes 7585792 | tf_op jit(solution)/shard_map/dot_general | solution.py:60
  43.3 0.0 copy-done.1
  43.3 3.2 %convolution_convert_fusion.1 = bf16[8,2,128,1152]{3,2,1,0:T(8,128)(2,1)S(1)} fusion(bf16[8,2,128,448]{2,3,1,0:T(8,128)(2,1)S(1)} %bitcast.33, bf16[448,1152]{1,0:T(8,128)(2,1)S(1)} %copy-done.1), kind=kOutput, calls=%fused_computation.2 | convolution fusion | flops 2116288512 | bytes 7585792 | tf_op jit(solution)/shard_map/dot_general | solution.py:59
  46.4 4.0 %maximum_bitcast_fusion = bf16[2,8,128,2304]{3,2,0,1:T(8,128)(2,1)} fusion(bf16[8,2,128,1152]{3,2,1,0:T(8,128)(2,1)S(1)} %convolution_convert_fusion, bf16[8,2,128,1152]{3,2,1,0:T(8,128)(2,1)S(1)} %convolution_convert_fusion.1), kind=kLoop, calls=%fused_computation | loop fusion | flops 18874368 | bytes 18874368 | tf_op jit(solution)/shard_map/transpose | solution.py:28
  50.5 8.1 %copy.7 = bf16[2,8,128,2304]{3,2,1,0:T(8,128)(2,1)} copy(bf16[2,8,128,2304]{3,2,0,1:T(8,128)(2,1)} %maximum_bitcast_fusion) | data formatting | bytes 18874368 | tf_op jit(solution)/shard_map/transpose | solution.py:28
  58.6 0.0 reduce-scatter.3.cloned.1.call-update
  58.6 0.0 copy-start.2
  58.6 0.0 reduce-scatter.5.cloned.1.call-start
  58.7 23.4 %reduce-scatter.3.cloned.1.call-done = bf16[8,128,2304]{2,1,0:T(8,128)(2,1)} async-done(((bf16[16,128,2304]{2,1,0:T(8,128)(2,1)}), bf16[8,128,2304]{2,1,0:T(8,128)(2,1)}) %reduce-scatter.3.cloned.1.call-update) | async-done | bytes 4718608 | tf_op jit(solution)/shard_map/reduce_scatter | solution.py:31
  82.1 0.0 reduce-scatter.5.cloned.1.call-update
  82.1 0.0 all-gather.2.cloned.1.call-start
  82.1 63.5 %reduce-scatter.5.cloned.1.call-done = bf16[1,128,2304]{2,1,0:T(8,128)(2,1)} async-done(((bf16[8,128,2304]{2,1,0:T(8,128)(2,1)}), bf16[1,128,2304]{2,1,0:T(8,128)(2,1)}) %reduce-scatter.5.cloned.1.call-update) | async-done | bytes 589840 | tf_op jit(solution)/shard_map/reduce_scatter | solution.py:31
  145.7 1.1 bitcast_convert_fusion
  146.8 0.9 fusion.3
  147.7 0.0 all-gather.2.cloned.1.call-update
  147.7 41.5 %all-gather.2.cloned.1.call-done = bf16[2048,1152]{1,0:T(8,128)(2,1)} async-done(((bf16[128,1152]{1,0:T(8,128)(2,1)}), bf16[2048,1152]{1,0:T(8,128)(2,1)}) %all-gather.2.cloned.1.call-update) | async-done | bytes 4718608 | tf_op jit(solution)/shard_map/all_gather | solution.py:66
  189.2 0.0 copy-done.2
  189.2 4.9 %fusion = bf16[56,16,8,128]{3,2,1,0:T(8,128)(2,1)S(1)} fusion(bf16[2048,1152]{1,0:T(8,128)(2,1)} %all-gather.2.cloned.1.call-done, bf16[1152,448]{0,1:T(8,128)(2,1)S(1)} %copy-done.2), kind=kOutput, calls=%fused_computation.5 | convolution fusion | flops 2114846720 | bytes 7585792 | tf_op jit(solution)/shard_map/dot_general | solution.py:65
  194.1 0.5 copy.13
  194.6 31.5 %all_to_all.11 = bf16[16,128,448]{1,2,0:T(8,128)(2,1)S(1)} all-to-all(bf16[16,128,448]{1,2,0:T(8,128)(2,1)S(1)} %bitcast.31), channel_id=1, replica_groups=mesh['row_0'=8,'row_1'=2,'col'=16] {'col'}, dimensions={0} | all-to-all | bytes 3670016 | tf_op jit(solution)/shard_map/all_to_all | solution.py:47
  226.1 0.9 reduce_sum.12
Async XLA Ops:
  6.5 33.6 %copy-start = (bf16[448,1152]{1,0:T(8,128)(2,1)S(1)}, bf16[448,1152]{1,0:T(8,128)(2,1)}, u32[]{:S(2)}) copy-start(bf16[448,1152]{1,0:T(8,128)(2,1)} %param.8) | copy-start | bytes 3096580
  6.5 75.5 %reduce-scatter.3.cloned.1.call-start = ((), (), s32[]{:S(2)}) async-start(), calls=%async_computation.4 | async-start | bytes 14155776 | tf_op jit(solution)/shard_map/reduce_scatter | solution.py:31
  40.1 3.2 %copy-start.1 = (bf16[448,1152]{1,0:T(8,128)(2,1)S(1)}, bf16[448,1152]{1,0:T(8,128)(2,1)}, u32[]{:S(2)}) copy-start(bf16[448,1152]{1,0:T(8,128)(2,1)} %param.7) | copy-start | bytes 3096580
  58.6 130.6 %copy-start.2 = (bf16[1152,448]{0,1:T(8,128)(2,1)S(1)}, bf16[1152,448]{0,1:T(8,128)(2,1)}, u32[]{:S(2)}) copy-start(bf16[1152,448]{0,1:T(8,128)(2,1)} %param.9) | copy-start | bytes 3096580
  58.6 87.0 %reduce-scatter.5.cloned.1.call-start = ((), (), s32[]{:S(2)}) async-start(), calls=%async_computation.5 | async-start | bytes 5308416 | tf_op jit(solution)/shard_map/reduce_scatter | solution.py:31
  82.1 107.1 %all-gather.2.cloned.1.call-start = ((), (), s32[]{:S(2)}) async-start(), calls=%async_computation.6 | async-start | bytes 5013504 | tf_op jit(solution)/shard_map/all_gather | solution.py:66
Sparse Core Ops, SparseCore 0:
  58.7 23.2 reduce-scatter.2
  84.6 60.9 reduce-scatter.4
  147.9 41.2 all-gather.1
where the time goes:
time: 234 us; the launch traced here: 233 us
  waiting for transfers between devices  128 us (55%)
  blocking collectives  63.6 us (27%)
  between operations  13.2 us (6%)
  matrix products  11.2 us (5%)
  local copies, waits for them, and re-layouts  8.97 us (4%)
  other arithmetic  8.02 us (3%)
    reduce_scatter x2, waiting for transfers between devices, own_block(): tiles = lax.psum_scatter(tiles, axes[k], scatter_dimension=0, tiled=True)  86.9 us
    all_gather x1, waiting for transfers between devices, on_device(): lax.all_gather(hidden, ROW, axis=0, tiled=True)  41.5 us
    all_to_all x1, blocking collectives, sent_to_all(): return lax.all_to_all(copies, axis, split_axis=0, concat_axis=0, tiled=True)  32.1 us
    all_to_all x1, blocking collectives, sent_and_summed(): lax.all_to_all(cut_along(array, dim, length), axis, 0, 0, tiled=True)  31.5 us
    transpose x1, local copies, waits for them, and re-layouts, own_block(): tiles = tiles.transpose(*order, *range(len(axes), tiles.ndim))  8.14 us
    dot_general x1, matrix products, on_device(): jnp.dot(lax.all_gather(hidden, ROW, axis=0, tiled=True), down_weight, pre...  4.9 us
  transfers between devices with their start and end apart: 3, of which 3 were waited for; matrix products, arithmetic and copies ran while one was open for 0% of the time, Pallas kernels for 0%

commit v1 on v0

--- a/solution.py
+++ b/solution.py
@@ -63,7 +63,9 @@
     ).astype(jnp.float32)
     hidden = (jax.nn.silu(summed[:, :hidden_width]) * summed[:, hidden_width:]).astype(jnp.bfloat16)
     partial_value = jnp.dot(
-        lax.all_gather(hidden, ROW, axis=0, tiled=True),
+        jnp.concatenate(
+            lax.all_to_all(jnp.stack([hidden] * lax.axis_size(ROW)), ROW, 0, 0), axis=0
+        ),
         down_weight,
         preferred_element_type=jnp.float32,
     )

time: 234 us -> 303 us (1.29)
  blocking collectives: 63.6 us -> 176 us
  waiting for transfers between devices: 128 us -> 87 us
    all_to_all x0 -> x1, blocking collectives: none -> 112 us  [on_device(): lax.all_to_all(jnp.stack([hidden] * lax.axis_size(ROW)), ROW, 0, 0)]
    all_gather x1 -> x0, waiting for transfers between devices: 41.5 us -> none  [on_device(): lax.all_gather(hidden, ROW, axis=0, tiled=True)]
  transfers between devices with their start and end apart: 3 -> 2, of which waited for: 3 -> 2; matrix products, arithmetic and copies ran while one was open for 0% -> 0% of each run, Pallas kernels for 0% -> 0%
where the time goes in v1:
time: 303 us; the launch traced here: 302 us
  blocking collectives  176 us (58%)
  waiting for transfers between devices  87 us (29%)
  between operations  13.5 us (4%)
  local copies, waits for them, and re-layouts  9.59 us (3%)
  matrix products  8.9 us (3%)
  other arithmetic  7.31 us (2%)
    all_to_all x1, blocking collectives, on_device(): lax.all_to_all(jnp.stack([hidden] * lax.axis_size(ROW)), ROW, 0, 0)  112 us
    reduce_scatter x2, waiting for transfers between devices, own_block(): tiles = lax.psum_scatter(tiles, axes[k], scatter_dimension=0, tiled=True)  87 us
    all_to_all x1, blocking collectives, sent_to_all(): return lax.all_to_all(copies, axis, split_axis=0, concat_axis=0, tiled=True)  32.1 us
    all_to_all x1, blocking collectives, sent_and_summed(): lax.all_to_all(cut_along(array, dim, length), axis, 0, 0, tiled=True)  31.8 us
    transpose x1, local copies, waits for them, and re-layouts, own_block(): tiles = tiles.transpose(*order, *range(len(axes), tiles.ndim))  8.13 us
  transfers between devices with their start and end apart: 2, of which 2 were waited for; matrix products, arithmetic and copies ran while one was open for 0% of the time, Pallas kernels for 0%

profile of v1, /device:TPU:1, one launch (start us, length us, event | category | flops | bytes accessed | tf_op | source)
XLA Modules:
  0.0 302.4 jit_solution(16204802959289999047)
XLA Ops:
  6.5 0.0 copy-start
  6.5 0.0 reduce-scatter.3.cloned.1.call-start
  6.5 1.1 fusion.4
  7.6 0.3 broadcast_in_dim.4
  8.0 32.1 %all_to_all.15 = bf16[16,128,448]{1,2,0:T(8,128)(2,1)S(1)} all-to-all(bf16[16,128,448]{1,2,0:T(8,128)(2,1)S(1)} %broadcast_in_dim.4), channel_id=1, replica_groups=mesh['row_0'=8,'row_1'=2,'col'=16] {'col'}, dimensions={0} | all-to-all | bytes 3670016 | tf_op jit(solution)/shard_map/all_to_all | solution.py:18
  40.1 0.0 copy-start.1
  40.1 0.0 copy-done
  40.1 3.2 %convolution_convert_fusion = bf16[8,2,128,1152]{3,2,1,0:T(8,128)(2,1)S(1)} fusion(bf16[8,2,128,448]{2,3,1,0:T(8,128)(2,1)S(1)} %bitcast.34, bf16[448,1152]{1,0:T(8,128)(2,1)S(1)} %copy-done), kind=kOutput, calls=%fused_computation.1 | convolution fusion | flops 2116288512 | bytes 7585792 | tf_op jit(solution)/shard_map/dot_general | solution.py:60
  43.3 0.0 copy-done.1
  43.3 3.2 %convolution_convert_fusion.1 = bf16[8,2,128,1152]{3,2,1,0:T(8,128)(2,1)S(1)} fusion(bf16[8,2,128,448]{2,3,1,0:T(8,128)(2,1)S(1)} %bitcast.35, bf16[448,1152]{1,0:T(8,128)(2,1)S(1)} %copy-done.1), kind=kOutput, calls=%fused_computation.2 | convolution fusion | flops 2116288512 | bytes 7585792 | tf_op jit(solution)/shard_map/dot_general | solution.py:59
  46.4 4.0 %maximum_bitcast_fusion = bf16[2,8,128,2304]{3,2,0,1:T(8,128)(2,1)} fusion(bf16[8,2,128,1152]{3,2,1,0:T(8,128)(2,1)S(1)} %convolution_convert_fusion, bf16[8,2,128,1152]{3,2,1,0:T(8,128)(2,1)S(1)} %convolution_convert_fusion.1), kind=kLoop, calls=%fused_computation | loop fusion | flops 18874368 | bytes 18874368 | tf_op jit(solution)/shard_map/transpose | solution.py:28
  50.5 8.1 %copy.7 = bf16[2,8,128,2304]{3,2,1,0:T(8,128)(2,1)} copy(bf16[2,8,128,2304]{3,2,0,1:T(8,128)(2,1)} %maximum_bitcast_fusion) | data formatting | bytes 18874368 | tf_op jit(solution)/shard_map/transpose | solution.py:28
  58.6 0.0 reduce-scatter.3.cloned.1.call-update
  58.6 0.0 reduce-scatter.5.cloned.1.call-start
  58.7 23.4 %reduce-scatter.3.cloned.1.call-done = bf16[8,128,2304]{2,1,0:T(8,128)(2,1)} async-done(((bf16[16,128,2304]{2,1,0:T(8,128)(2,1)}), bf16[8,128,2304]{2,1,0:T(8,128)(2,1)}) %reduce-scatter.3.cloned.1.call-update) | async-done | bytes 4718608 | tf_op jit(solution)/shard_map/reduce_scatter | solution.py:31
  82.1 0.0 reduce-scatter.5.cloned.1.call-update
  82.1 63.6 %reduce-scatter.5.cloned.1.call-done = bf16[1,128,2304]{2,1,0:T(8,128)(2,1)} async-done(((bf16[8,128,2304]{2,1,0:T(8,128)(2,1)}), bf16[1,128,2304]{2,1,0:T(8,128)(2,1)}) %reduce-scatter.5.cloned.1.call-update) | async-done | bytes 589840 | tf_op jit(solution)/shard_map/reduce_scatter | solution.py:31
  145.7 1.1 bitcast_convert_fusion
  146.8 0.2 fusion.3
  147.0 0.6 stack.2
  147.6 0.0 copy-start.2
  147.6 112.1 %all_to_all.16 = bf16[16,128,1152]{2,1,0:T(8,128)(2,1)S(1)} all-to-all(bf16[16,128,1152]{2,1,0:T(8,128)(2,1)S(1)} %stack.2), channel_id=1, replica_groups=mesh['row_0'=8,'row_1'=2,'col'=16] {'row_0','row_1'}, dimensions={0} | all-to-all | bytes 9437184 | tf_op jit(solution)/shard_map/all_to_all | solution.py:67
  259.8 0.0 copy-done.2
  259.8 2.6 fusion
  262.3 0.5 copy.13
  262.8 31.8 %all_to_all.17 = bf16[16,128,448]{1,2,0:T(8,128)(2,1)S(1)} all-to-all(bf16[16,128,448]{1,2,0:T(8,128)(2,1)S(1)} %bitcast.32), channel_id=1, replica_groups=mesh['row_0'=8,'row_1'=2,'col'=16] {'col'}, dimensions={0} | all-to-all | bytes 3670016 | tf_op jit(solution)/shard_map/all_to_all | solution.py:47
  294.6 0.9 reduce_sum.12
Async XLA Ops:
  6.5 33.6 %copy-start = (bf16[448,1152]{1,0:T(8,128)(2,1)S(1)}, bf16[448,1152]{1,0:T(8,128)(2,1)}, u32[]{:S(2)}) copy-start(bf16[448,1152]{1,0:T(8,128)(2,1)} %param.8) | copy-start | bytes 3096580
  6.5 75.5 %reduce-scatter.3.cloned.1.call-start = ((), (), s32[]{:S(2)}) async-start(), calls=%async_computation.5 | async-start | bytes 14155776 | tf_op jit(solution)/shard_map/reduce_scatter | solution.py:31
  40.1 3.2 %copy-start.1 = (bf16[448,1152]{1,0:T(8,128)(2,1)S(1)}, bf16[448,1152]{1,0:T(8,128)(2,1)}, u32[]{:S(2)}) copy-start(bf16[448,1152]{1,0:T(8,128)(2,1)} %param.7) | copy-start | bytes 3096580
  58.6 87.0 %reduce-scatter.5.cloned.1.call-start = ((), (), s32[]{:S(2)}) async-start(), calls=%async_computation.6 | async-start | bytes 5308416 | tf_op jit(solution)/shard_map/reduce_scatter | solution.py:31
  147.6 112.1 %copy-start.2 = (bf16[1152,448]{0,1:T(8,128)(2,1)S(1)}, bf16[1152,448]{0,1:T(8,128)(2,1)}, u32[]{:S(2)}) copy-start(bf16[1152,448]{0,1:T(8,128)(2,1)} %param.9) | copy-start | bytes 3096580
Sparse Core Ops, SparseCore 0:
  58.7 23.2 reduce-scatter.2
  84.6 60.9 reduce-scatter.4
